TPU v7x, 32 devices: a whole 2x2x4 slice. The times are simulated.
32 devices in a mesh: section: 4 (over y, core), sim: 8 (over z, x).
Axes of the slice: x: 2, y: 2, z: 4, core: 2. Of those that a mesh axis runs over, the one named last changes fastest.
Arguments:
- state: float32 [128, 64, 8192], P('section', None, 'sim'), may hold values from -60 to 60
- owner: int32 [128, 1], P('section'), may hold values from 0 to 7; in each aligned block of 32 rows (0 to 31, 32 to 63, ...) at most 8 rows name the same one
- counts: int32 [128], P('section'), may hold values from 2048 to 8192
Outputs:
- slab_mean: float32 [128, 64], P('section')
- slab_cov: float32 [128, 4096], P('section', 'sim')
- group_cov: float32 [32, 4096], P(('section', 'sim'))
- global_mean: float32 [64], replicated
- global_cov: float32 [64, 64], replicated
Inputs may be any that keep to these rules, and one draw needn't show every extreme that they name: Among the 32 slabs of one group, no owner is named by more than 8 slabs, and one owner is named by exactly 8 slabs in some or all groups.
All inputs are finite; a program needn't handle non-finite values.
Results may differ from a plain program's by a relative error of at most 0.0003.
Values sent between devices are 32-bit elements; how exact they have to be, the bound alone decides.
A program may use at most 64 MiB of HBM per device.

v0:
```python
import jax
import jax.numpy as jnp
from jax import lax
from jax.sharding import PartitionSpec as P


def slot_payload(number, mean, comoment, capacity, n_sim, width):
    slot_cov = comoment / jnp.maximum(number - 1.0, 1.0)[:, None]
    cov_parts = slot_cov.reshape(capacity, n_sim, width * width // n_sim)
    mean_copies = jnp.broadcast_to(mean[:, None, :], (capacity, n_sim, width))
    return (cov_parts, mean_copies)


def owner_stats(number, mean, comoment):
    high = lax.Precision.HIGHEST
    width = mean.shape[1]
    group_count = jnp.sum(number)
    group_mean = jnp.sum(number[:, None] * mean, axis=0) / jnp.maximum(group_count, 1.0)
    offset = mean - group_mean[None, :]
    group_co = jnp.sum(comoment, axis=0) + jnp.einsum(
        "k,kv,kw->vw", number, offset, offset, precision=high
    ).reshape(width * width)
    return (group_count, group_mean, group_co)


def local(state, owner, counts):
    high = lax.Precision.HIGHEST
    slab_here, width, cells_dev = state.shape
    n_sim = lax.axis_size("sim")
    my_index = lax.axis_index("sim")
    capacity = 2 * slab_here // n_sim
    slots = n_sim * capacity
    target = owner[:, 0]
    order = jnp.arange(slab_here, dtype=jnp.int32)
    earlier = (target[:, None] == target[None, :]) & (order[None, :] < order[:, None])
    rank = jnp.sum(earlier.astype(jnp.int32), axis=1)
    slot_of = target * capacity + rank
    match = slot_of[:, None] == jnp.arange(slots, dtype=jnp.int32)[None, :]
    filled = jnp.any(match, axis=0)
    source_slab = jnp.sum(jnp.where(match, order[:, None], 0), axis=0)
    tile_start = my_index * cells_dev
    tile_count = jnp.clip(counts - tile_start, 0, cells_dev).astype(jnp.float32)
    live = jnp.arange(cells_dev, dtype=jnp.int32)[None, :] + tile_start < counts[:, None]
    tile_mean = (
        jnp.sum(jnp.where(live[:, None, :], state, 0.0), axis=2)
        / jnp.maximum(tile_count, 1.0)[:, None]
    )
    centered = jnp.where(live[:, None, :], state - tile_mean[:, :, None], 0.0)
    tile_co = jnp.einsum("svc,swc->svw", centered, centered, precision=high).reshape(
        slab_here, width * width
    )
    send_mean = jnp.where(filled[:, None], tile_mean[source_slab], 0.0).reshape(
        n_sim, capacity, width
    )
    send_co = jnp.where(filled[:, None], tile_co[source_slab], 0.0).reshape(
        n_sim, capacity, width * width
    )
    send_count = jnp.where(filled, tile_count[source_slab], 0.0).reshape(n_sim, capacity)
    means = lax.all_to_all(send_mean, "sim", split_axis=0, concat_axis=0, tiled=True)
    comoms = lax.all_to_all(send_co, "sim", split_axis=0, concat_axis=0, tiled=True)
    amounts = lax.all_to_all(send_count, "sim", split_axis=0, concat_axis=0, tiled=True)
    number = jnp.sum(amounts, axis=0)
    mean = jnp.sum(amounts[:, :, None] * means, axis=0) / jnp.maximum(number, 1.0)[:, None]
    offset = means - mean[None, :, :]
    extra = jnp.einsum("ik,ikv,ikw->kvw", amounts, offset, offset, precision=high)
    number, mean, comoment = (
        number,
        mean,
        jnp.sum(comoms, axis=0) + extra.reshape(number.shape[0], width * width),
    )
    cov_parts, mean_copies = slot_payload(number, mean, comoment, capacity, n_sim, width)
    back_cov, back_mean = (
        lax.all_to_all(cov_parts, "sim", split_axis=1, concat_axis=0, tiled=True),
        lax.all_to_all(mean_copies, "sim", split_axis=1, concat_axis=0, tiled=True),
    )
    slab_cov = back_cov[slot_of, 0]
    slab_mean = back_mean[slot_of, 0]
    group_count, group_mean, group_co = owner_stats(number, mean, comoment)
    group_cov = (group_co / jnp.maximum(group_count - 1.0, 1.0))[None, :]
    total, weighted = lax.psum((group_count, group_count * group_mean), ("section", "sim"))
    global_mean = weighted / total
    gap = group_mean - global_mean
    spread = lax.psum(group_co + group_count * jnp.outer(gap, gap).reshape(-1), ("section", "sim"))
    global_cov = (spread / (total - 1.0)).reshape(width, width)
    return (slab_mean, slab_cov, group_cov, global_mean, global_cov)


def solution(mesh):
    return jax.shard_map(
        local,
        mesh=mesh,
        in_specs=(P("section", None, "sim"), P("section", None), P("section")),
        out_specs=(P("section", None), P("section", "sim"), P(("section", "sim"), None), P(), P()),
        check_vma=False,
    )
```

profile of v0, /device:TPU:0, one launch (start us, length us, event | category | flops | bytes accessed | tf_op | source)
XLA Modules:
  0.0 160.8 jit_solution(15916009984353185825)
XLA Ops:
  0.6 0.9 convert_reduce_fusion
  1.5 0.7 fusion.19
  2.4 0.7 broadcast_maximum_fusion.1
  3.1 0.8 gather_fusion
  3.9 0.7 select_n.56
  4.5 7.3 %all-to-all-start = ((f32[8,1,8]{2,1,0:T(1,128)}), f32[8,1,8]{2,1,0:T(1,128)S(1)}, u32[]{:S(2)}, u32[]{:S(2)}) async-start(f32[8,1,8]{2,1,0:T(1,128)} %bitcast.5), calls=%async_computation | async-start | bytes 8192 | tf_op jit(solution)/shard_map/all_to_all | solution.py:61
  11.9 0.7 broadcast_compare_fusion
  12.7 4.1 %select_reduce_fusion = f32[32,64]{1,0:T(8,128)S(1)} fusion(f32[32,64,1024]{2,1,0:T(8,128)} %param.3, pred[32,1024]{1,0:T(8,128)(4,1)S(1)} %broadcast_compare_fusion), kind=kLoop, calls=%fused_computation.8 | loop fusion | flops 4192256 | bytes 8429568 | tf_op jit(solution)/shard_map/reduce_sum | solution.py:45
  17.5 14.9 %fusion = f32[32,64,64]{2,1,0:T(8,128)S(1)} fusion(f32[32,64,1024]{2,1,0:T(8,128)} %param.3, f32[32,64]{1,0:T(8,128)S(1)} %broadcast_divide_fusion.2, pred[32,1024]{1,0:T(8,128)(4,1)S(1)} %broadcast_compare_fusion), kind=kOutput, calls=%fused_computation.5 | convolution fusion | flops 1614807040 | bytes 8953856 | tf_op jit(solution)/shard_map/svc,swc->svw/dot_general | solution.py:49
  32.5 0.7 reshape.244
  33.5 0.9 gather_fusion.3
  34.5 6.0 %all-to-all-start.1 = ((f32[8,1,512]{2,1,0:T(1,128)}), f32[8,1,512]{2,1,0:T(1,128)S(1)}, u32[]{:S(2)}, u32[]{:S(2)}) async-start(f32[8,1,512]{2,1,0:T(1,128)} %reshape.244), calls=%async_computation.1 | async-start | bytes 32768 | tf_op jit(solution)/shard_map/all_to_all | solution.py:59
  41.1 6.0 %all-to-all-done.1 = f32[8,1,512]{2,1,0:T(1,128)S(1)} async-done(((f32[8,1,512]{2,1,0:T(1,128)}), f32[8,1,512]{2,1,0:T(1,128)S(1)}, u32[]{:S(2)}, u32[]{:S(2)}) %all-to-all-start.1) | async-done | bytes 16416 | tf_op jit(solution)/shard_map/all_to_all | solution.py:59
  47.6 0.7 reduce.4
  48.5 0.7 reshape.246
  49.2 3.3 %all-to-all-start.2 = ((f32[8,1,512]{2,1,0:T(1,128)}), f32[8,1,512]{2,1,0:T(1,128)S(1)}, u32[]{:S(2)}, u32[]{:S(2)}) async-start(f32[8,1,512]{2,1,0:T(1,128)} %reshape.246), calls=%async_computation.2 | async-start | bytes 32768 | tf_op jit(solution)/shard_map/all_to_all | solution.py:74
  52.6 1.1 bitcast_select_fusion
  53.7 5.4 %all-to-all-done.2 = f32[8,1,512]{2,1,0:T(1,128)S(1)} async-done(((f32[8,1,512]{2,1,0:T(1,128)}), f32[8,1,512]{2,1,0:T(1,128)S(1)}, u32[]{:S(2)}, u32[]{:S(2)}) %all-to-all-start.2) | async-done | bytes 16416 | tf_op jit(solution)/shard_map/all_to_all | solution.py:74
  59.1 3.6 %all-to-all-start.3 = ((f32[8,8,4096]{2,1,0:T(8,128)}), f32[8,8,4096]{2,1,0:T(8,128)S(1)}, u32[]{:S(2)}, u32[]{:S(2)}) async-start(f32[8,8,4096]{2,1,0:T(8,128)} %bitcast_select_fusion), calls=%async_computation.3 | async-start | bytes 2097152 | tf_op jit(solution)/shard_map/all_to_all | solution.py:60
  63.9 0.7 broadcast_multiply_fusion.1
  64.6 41.6 %all-reduce.1 = (f32[64]{0:T(128)S(1)}, f32[]{:T(128)}) all-reduce(f32[64]{0:T(128)S(1)} %get-tuple-element.11, f32[]{:T(128)} %get-tuple-element.5), channel_id=1, replica_groups=mesh['section'=4,'sim'=8] {'section','sim'}, use_global_device_ids=true, to_apply=%region_10.11 | all-reduce | flops 65 | bytes 520 | tf_op jit(solution)/shard_map/psum | solution.py:80
  106.8 1.2 fusion.23
  108.1 0.7 reduce.5
  108.8 1.2 gather_fusion.2
  110.2 0.6 add_reduce_fusion
  110.9 0.7 fusion.6
  111.7 5.3 %all-to-all-start.4 = ((f32[8,8,512]{2,0,1:T(8,128)}), f32[8,8,512]{2,0,1:T(8,128)S(1)}, u32[]{:S(2)}, u32[]{:S(2)}) async-start(f32[8,8,512]{2,0,1:T(8,128)} %fusion.6), calls=%async_computation.4 | async-start | bytes 262144 | tf_op jit(solution)/shard_map/all_to_all | solution.py:73
  117.0 1.0 multiply_add_fusion
  117.9 0.7 div.85
  118.7 40.0 %psum.23 = f32[4096]{0:T(1024)S(1)} all-reduce(f32[4096]{0:T(1024)S(1)} %add.82), channel_id=1, replica_groups=mesh['section'=4,'sim'=8] {'section','sim'}, use_global_device_ids=true, to_apply=%region_12.13 | all-reduce | flops 4096 | bytes 32768 | tf_op jit(solution)/shard_map/psum | solution.py:83
  158.7 0.7 reshape.207
  159.6 1.2 gather_fusion.4
  (29 shorter events, 3.4 us)
Async XLA Ops:
  4.5 29.9 %all-to-all-start = ((f32[8,1,8]{2,1,0:T(1,128)}), f32[8,1,8]{2,1,0:T(1,128)S(1)}, u32[]{:S(2)}, u32[]{:S(2)}) async-start(f32[8,1,8]{2,1,0:T(1,128)} %bitcast.5), calls=%async_computation | async-start | bytes 8192 | tf_op jit(solution)/shard_map/all_to_all | solution.py:61
  34.5 12.6 %all-to-all-start.1 = ((f32[8,1,512]{2,1,0:T(1,128)}), f32[8,1,512]{2,1,0:T(1,128)S(1)}, u32[]{:S(2)}, u32[]{:S(2)}) async-start(f32[8,1,512]{2,1,0:T(1,128)} %reshape.244), calls=%async_computation.1 | async-start | bytes 32768 | tf_op jit(solution)/shard_map/all_to_all | solution.py:59
  49.2 9.9 %all-to-all-start.2 = ((f32[8,1,512]{2,1,0:T(1,128)}), f32[8,1,512]{2,1,0:T(1,128)S(1)}, u32[]{:S(2)}, u32[]{:S(2)}) async-start(f32[8,1,512]{2,1,0:T(1,128)} %reshape.246), calls=%async_computation.2 | async-start | bytes 32768 | tf_op jit(solution)/shard_map/all_to_all | solution.py:74
  59.1 51.0 %all-to-all-start.3 = ((f32[8,8,4096]{2,1,0:T(8,128)}), f32[8,8,4096]{2,1,0:T(8,128)S(1)}, u32[]{:S(2)}, u32[]{:S(2)}) async-start(f32[8,8,4096]{2,1,0:T(8,128)} %bitcast_select_fusion), calls=%async_computation.3 | async-start | bytes 2097152 | tf_op jit(solution)/shard_map/all_to_all | solution.py:60
  111.7 47.8 %all-to-all-start.4 = ((f32[8,8,512]{2,0,1:T(8,128)}), f32[8,8,512]{2,0,1:T(8,128)S(1)}, u32[]{:S(2)}, u32[]{:S(2)}) async-start(f32[8,8,512]{2,0,1:T(8,128)} %fusion.6), calls=%async_computation.4 | async-start | bytes 262144 | tf_op jit(solution)/shard_map/all_to_all | solution.py:73
where the time goes:
time: 162 us; the launch traced here: 161 us
  blocking collectives  81.6 us (50%)
  starting transfers between devices  25.5 us (16%)
  matrix products  16.5 us (10%)
  other arithmetic  13.4 us (8%)
  waiting for transfers between devices  11.3 us (7%)
  local copies, waits for them, and re-layouts  9.73 us (6%)
  between operations  2.71 us (2%)
    psum x1, blocking collectives, local(): lax.psum((group_count, group_count * group_mean), ('section', 'sim'))  41.6 us
    psum x1, blocking collectives, local(): lax.psum(group_co + group_count * jnp.outer(gap, gap).reshape(-1), ('sect...  40 us
    dot_general x1, matrix products, local(): jnp.einsum('svc,swc->svw', centered, centered, precision=high)  14.9 us
    all_to_all x1, starting transfers between devices, local(): lax.all_to_all(send_count, 'sim', split_axis=0, concat_axis=0, tiled=True)  7.28 us
    all_to_all x1, starting transfers between devices, local(): lax.all_to_all(send_mean, 'sim', split_axis=0, concat_axis=0, tiled=True)  6.01 us
    all_to_all x1, waiting for transfers between devices, local(): lax.all_to_all(send_mean, 'sim', split_axis=0, concat_axis=0, tiled=True)  5.96 us
    all_to_all x1, waiting for transfers between devices, local(): lax.all_to_all(mean_copies, 'sim', split_axis=1, concat_axis=0, tiled=True)  5.37 us
    all_to_all x1, starting transfers between devices, local(): lax.all_to_all(cov_parts, 'sim', split_axis=1, concat_axis=0, tiled=True)  5.31 us
  transfers between devices with their start and end apart: 5, of which 2 were waited for; matrix products, arithmetic and copies ran while one was open for 19% of the time, Pallas kernels for 0%

commit v1 on v0

--- a/solution.py
+++ b/solution.py
@@ -80,7 +80,12 @@
     total, weighted = lax.psum((group_count, group_count * group_mean), ("section", "sim"))
     global_mean = weighted / total
     gap = group_mean - global_mean
-    spread = lax.psum(group_co + group_count * jnp.outer(gap, gap).reshape(-1), ("section", "sim"))
+    spread = jnp.sum(
+        lax.all_gather(
+            group_co + group_count * jnp.outer(gap, gap).reshape(-1), ("section", "sim")
+        ),
+        axis=0,
+    )
     global_cov = (spread / (total - 1.0)).reshape(width, width)
     return (slab_mean, slab_cov, group_cov, global_mean, global_cov)
 

time: 162 us -> 191 us (1.18)
  blocking collectives: 81.6 us -> 111 us
    all_gather x0 -> x1, blocking collectives: none -> 69.1 us  [local(): lax.all_gather(group_co + group_count * jnp.outer(gap, gap).reshape(-1),...]
    psum x1 -> x0, blocking collectives: 40 us -> none  [local(): lax.psum(group_co + group_count * jnp.outer(gap, gap).reshape(-1), ('sect...]
  transfers between devices with their start and end apart: 5 -> 5, of which waited for: 2 -> 2; matrix products, arithmetic and copies ran while one was open for 19% -> 16% of each run, Pallas kernels for 0% -> 0%
where the time goes in v1:
time: 191 us; the launch traced here: 190 us
  blocking collectives  111 us (58%)
  starting transfers between devices  25.5 us (13%)
  matrix products  16.5 us (9%)
  other arithmetic  13.8 us (7%)
  waiting for transfers between devices  11.3 us (6%)
  local copies, waits for them, and re-layouts  9.74 us (5%)
  between operations  2.72 us (1%)
    all_gather x1, blocking collectives, local(): lax.all_gather(group_co + group_count * jnp.outer(gap, gap).reshape(-1),...  69.1 us
    psum x1, blocking collectives, local(): lax.psum((group_count, group_count * group_mean), ('section', 'sim'))  41.6 us
    dot_general x1, matrix products, local(): jnp.einsum('svc,swc->svw', centered, centered, precision=high)  14.9 us
    all_to_all x1, starting transfers between devices, local(): lax.all_to_all(send_count, 'sim', split_axis=0, concat_axis=0, tiled=True)  7.28 us
    all_to_all x1, starting transfers between devices, local(): lax.all_to_all(send_mean, 'sim', split_axis=0, concat_axis=0, tiled=True)  6.01 us
    all_to_all x1, waiting for transfers between devices, local(): lax.all_to_all(send_mean, 'sim', split_axis=0, concat_axis=0, tiled=True)  5.96 us
    all_to_all x1, waiting for transfers between devices, local(): lax.all_to_all(mean_copies, 'sim', split_axis=1, concat_axis=0, tiled=True)  5.37 us
    all_to_all x1, starting transfers between devices, local(): lax.all_to_all(cov_parts, 'sim', split_axis=1, concat_axis=0, tiled=True)  5.31 us
  transfers between devices with their start and end apart: 5, of which 2 were waited for; matrix products, arithmetic and copies ran while one was open for 16% of the time, Pallas kernels for 0%

profile of v1, /device:TPU:0, one launch (start us, length us, event | category | flops | bytes accessed | tf_op | source)
XLA Modules:
  0.0 190.2 jit_solution(1760976473713318403)
XLA Ops:
  0.6 0.9 convert_reduce_fusion
  1.5 0.7 fusion.19
  2.4 0.7 broadcast_maximum_fusion.1
  3.1 0.8 gather_fusion
  3.9 0.7 select_n.56
  4.5 7.3 %all-to-all-start = ((f32[8,1,8]{2,1,0:T(1,128)}), f32[8,1,8]{2,1,0:T(1,128)S(1)}, u32[]{:S(2)}, u32[]{:S(2)}) async-start(f32[8,1,8]{2,1,0:T(1,128)} %bitcast.5), calls=%async_computation | async-start | bytes 8192 | tf_op jit(solution)/shard_map/all_to_all | solution.py:61
  11.9 0.7 broadcast_compare_fusion
  12.7 4.1 %select_reduce_fusion = f32[32,64]{1,0:T(8,128)S(1)} fusion(f32[32,64,1024]{2,1,0:T(8,128)} %param.3, pred[32,1024]{1,0:T(8,128)(4,1)S(1)} %broadcast_compare_fusion), kind=kLoop, calls=%fused_computation.8 | loop fusion | flops 4192256 | bytes 8429568 | tf_op jit(solution)/shard_map/reduce_sum | solution.py:45
  17.5 14.9 %fusion = f32[32,64,64]{2,1,0:T(8,128)S(1)} fusion(f32[32,64,1024]{2,1,0:T(8,128)} %param.3, f32[32,64]{1,0:T(8,128)S(1)} %broadcast_divide_fusion.2, pred[32,1024]{1,0:T(8,128)(4,1)S(1)} %broadcast_compare_fusion), kind=kOutput, calls=%fused_computation.5 | convolution fusion | flops 1614807040 | bytes 8953856 | tf_op jit(solution)/shard_map/svc,swc->svw/dot_general | solution.py:49
  32.5 0.7 reshape.278
  33.5 0.9 gather_fusion.3
  34.5 6.0 %all-to-all-start.1 = ((f32[8,1,512]{2,1,0:T(1,128)}), f32[8,1,512]{2,1,0:T(1,128)S(1)}, u32[]{:S(2)}, u32[]{:S(2)}) async-start(f32[8,1,512]{2,1,0:T(1,128)} %reshape.278), calls=%async_computation.1 | async-start | bytes 32768 | tf_op jit(solution)/shard_map/all_to_all | solution.py:59
  41.1 6.0 %all-to-all-done.1 = f32[8,1,512]{2,1,0:T(1,128)S(1)} async-done(((f32[8,1,512]{2,1,0:T(1,128)}), f32[8,1,512]{2,1,0:T(1,128)S(1)}, u32[]{:S(2)}, u32[]{:S(2)}) %all-to-all-start.1) | async-done | bytes 16416 | tf_op jit(solution)/shard_map/all_to_all | solution.py:59
  47.6 0.7 reduce.5
  48.5 0.7 reshape.280
  49.2 3.3 %all-to-all-start.2 = ((f32[8,1,512]{2,1,0:T(1,128)}), f32[8,1,512]{2,1,0:T(1,128)S(1)}, u32[]{:S(2)}, u32[]{:S(2)}) async-start(f32[8,1,512]{2,1,0:T(1,128)} %reshape.280), calls=%async_computation.2 | async-start | bytes 32768 | tf_op jit(solution)/shard_map/all_to_all | solution.py:74
  52.6 1.1 bitcast_select_fusion
  53.7 5.4 %all-to-all-done.2 = f32[8,1,512]{2,1,0:T(1,128)S(1)} async-done(((f32[8,1,512]{2,1,0:T(1,128)}), f32[8,1,512]{2,1,0:T(1,128)S(1)}, u32[]{:S(2)}, u32[]{:S(2)}) %all-to-all-start.2) | async-done | bytes 16416 | tf_op jit(solution)/shard_map/all_to_all | solution.py:74
  59.1 3.6 %all-to-all-start.3 = ((f32[8,8,4096]{2,1,0:T(8,128)}), f32[8,8,4096]{2,1,0:T(8,128)S(1)}, u32[]{:S(2)}, u32[]{:S(2)}) async-start(f32[8,8,4096]{2,1,0:T(8,128)} %bitcast_select_fusion), calls=%async_computation.3 | async-start | bytes 2097152 | tf_op jit(solution)/shard_map/all_to_all | solution.py:60
  63.9 0.7 broadcast_multiply_fusion.1
  64.6 41.6 %all-reduce.1 = (f32[64]{0:T(128)S(1)}, f32[]{:T(128)}) all-reduce(f32[64]{0:T(128)S(1)} %get-tuple-element.11, f32[]{:T(128)} %get-tuple-element.5), channel_id=1, replica_groups=mesh['section'=4,'sim'=8] {'section','sim'}, use_global_device_ids=true, to_apply=%region_10.11 | all-reduce | flops 65 | bytes 520 | tf_op jit(solution)/shard_map/psum | solution.py:80
  106.8 1.2 fusion.23
  108.1 0.7 reduce.6
  108.8 1.2 gather_fusion.2
  110.2 0.6 add_reduce_fusion
  110.9 0.7 fusion.6
  111.7 5.3 %all-to-all-start.4 = ((f32[8,8,512]{2,0,1:T(8,128)}), f32[8,8,512]{2,0,1:T(8,128)S(1)}, u32[]{:S(2)}, u32[]{:S(2)}) async-start(f32[8,8,512]{2,0,1:T(8,128)} %fusion.6), calls=%async_computation.4 | async-start | bytes 262144 | tf_op jit(solution)/shard_map/all_to_all | solution.py:73
  117.0 1.0 multiply_add_fusion
  118.0 69.1 %all-gather = f32[32,1,4096]{2,1,0:T(1,128)S(1)} all-gather(f32[1,1,4096]{2,1,0:T(1,128)S(1)} %reshape.275), channel_id=1, replica_groups=mesh['section'=4,'sim'=8] {'section','sim'}, dimensions={0}, use_global_device_ids=true | all-gather | bytes 540672 | tf_op jit(solution)/shard_map/all_gather | solution.py:84
  187.1 0.7 div.89
  188.2 0.7 div.94
  189.0 1.2 gather_fusion.4
  (30 shorter events, 3.8 us)
Async XLA Ops:
  4.5 29.9 %all-to-all-start = ((f32[8,1,8]{2,1,0:T(1,128)}), f32[8,1,8]{2,1,0:T(1,128)S(1)}, u32[]{:S(2)}, u32[]{:S(2)}) async-start(f32[8,1,8]{2,1,0:T(1,128)} %bitcast.5), calls=%async_computation | async-start | bytes 8192 | tf_op jit(solution)/shard_map/all_to_all | solution.py:61
  34.5 12.6 %all-to-all-start.1 = ((f32[8,1,512]{2,1,0:T(1,128)}), f32[8,1,512]{2,1,0:T(1,128)S(1)}, u32[]{:S(2)}, u32[]{:S(2)}) async-start(f32[8,1,512]{2,1,0:T(1,128)} %reshape.278), calls=%async_computation.1 | async-start | bytes 32768 | tf_op jit(solution)/shard_map/all_to_all | solution.py:59
  49.2 9.9 %all-to-all-start.2 = ((f32[8,1,512]{2,1,0:T(1,128)}), f32[8,1,512]{2,1,0:T(1,128)S(1)}, u32[]{:S(2)}, u32[]{:S(2)}) async-start(f32[8,1,512]{2,1,0:T(1,128)} %reshape.280), calls=%async_computation.2 | async-start | bytes 32768 | tf_op jit(solution)/shard_map/all_to_all | solution.py:74
  59.1 51.0 %all-to-all-start.3 = ((f32[8,8,4096]{2,1,0:T(8,128)}), f32[8,8,4096]{2,1,0:T(8,128)S(1)}, u32[]{:S(2)}, u32[]{:S(2)}) async-start(f32[8,8,4096]{2,1,0:T(8,128)} %bitcast_select_fusion), calls=%async_computation.3 | async-start | bytes 2097152 | tf_op jit(solution)/shard_map/all_to_all | solution.py:60
  111.7 77.2 %all-to-all-start.4 = ((f32[8,8,512]{2,0,1:T(8,128)}), f32[8,8,512]{2,0,1:T(8,128)S(1)}, u32[]{:S(2)}, u32[]{:S(2)}) async-start(f32[8,8,512]{2,0,1:T(8,128)} %fusion.6), calls=%async_computation.4 | async-start | bytes 262144 | tf_op jit(solution)/shard_map/all_to_all | solution.py:73
